TPU v7x, 32 devices: a whole 2x2x4 slice. The times are simulated.
32 devices in a mesh: row: 4 (over x, core), col: 8 (over z, y).
Axes of the slice: x: 2, y: 2, z: 4, core: 2. Of those that a mesh axis runs over, the one named last changes fastest.
Arguments:
- hamiltonian: bfloat16 [2912, 2912], P('row', 'col'), may hold values from -6 to 6
- new_atom: int32 [224], replicated, may hold values from 0 to 223, as said below
- pattern: int32 [224, 224], P('row', 'col'), may hold values 0 or 1
Outputs:
- sign_matrix: float32 [2912, 2912], P('row', 'col')
Inputs may be any that keep to these rules, and one draw needn't show every extreme that they name: `new_atom`: each old atom appears once. Block column b holds atoms b * 28 to (b + 1) * 28 - 1 in both orders. For each new block column d and each v from 0 to 27, exactly one atom of new block column d comes from old block column (d - 1 - (v mod 8)) mod 8, so the number of atoms that old block column b sends to new block column (b + k) mod 8 is the number of such v with (1 + v) mod 8 = k.
All inputs are finite; a program needn't handle non-finite values. No bound on the sum of `pattern` on one device may be relied on, other than what follows from the above.
Results may differ from a plain program's by a relative error of at most 0.0029.
Values may be sent and summed in bfloat16 or wider, within the bound.
A program may use at most 64 MiB of HBM per device.

v0:
```python
import jax
import jax.numpy as jnp
from jax import lax
from jax.sharding import PartitionSpec as P

NBF = 13
BF = jnp.bfloat16
F32 = jnp.float32


def mm(a, b):
    return jnp.dot(a, b, preferred_element_type=F32)


def spread(n):
    i = lax.broadcasted_iota(jnp.int32, (n * NBF, n), 0)
    a = lax.broadcasted_iota(jnp.int32, (n * NBF, n), 1) * NBF
    return (i >= a) & (i < a + NBF)


def on_device(hamiltonian, new_atom, pattern):
    rows_here, cols_here = hamiltonian.shape
    order = rows_here * lax.axis_size("row")
    atoms = order // NBF
    ar, ac = pattern.shape
    row_here = lax.axis_index("row")
    col_here = lax.axis_index("col")
    panel = lax.all_gather(hamiltonian, "col", axis=1, tiled=True)
    pat = lax.all_gather(pattern.astype(BF), ("row", "col"), axis=0, tiled=False)
    n_row, n_col = (lax.axis_size("row"), lax.axis_size("col"))
    pat = pat.reshape(n_row, n_col, ar, ac).transpose(0, 2, 1, 3).reshape(atoms, atoms)
    old = jnp.arange(atoms, dtype=jnp.int32)
    perm = (new_atom[:, None] == old[None, :]).astype(BF)
    mine = (new_atom[None, :] == row_here * ar + jnp.arange(ar, dtype=jnp.int32)[:, None]).astype(
        BF
    )
    pat_rows = mm(mine, pat).astype(BF)
    e_row = spread(ar)
    e_col = spread(ac)
    e_rowb = e_row.astype(BF)
    rows_masked = mm(e_rowb, mm(pat_rows, perm).astype(BF)).astype(BF)
    keep = mm(rows_masked, spread(atoms).astype(BF).T).astype(BF)
    m = panel * keep
    total = lax.psum(jnp.sum(m.astype(F32) ** 2), "row")
    s = lax.rsqrt(total / order)

    def old_index(n, here, e):
        mine_atoms = lax.dynamic_slice_in_dim(new_atom, here * n, n)
        base = jnp.sum(
            jnp.where(e, (mine_atoms - jnp.arange(n, dtype=jnp.int32))[None, :], 0), axis=1
        )
        return base * NBF + jnp.arange(n * NBF, dtype=jnp.int32)

    full = jnp.arange(order, dtype=jnp.int32)
    pick_col = (full[:, None] == old_index(ac, col_here, e_col)[None, :]).astype(BF)
    pick_row = (old_index(ar, row_here, e_row)[:, None] == full[None, :]).astype(BF)
    right = lax.all_gather(mm(m, pick_col).astype(BF), "row", axis=0, tiled=True)
    e_colt = e_col.astype(BF).T
    here_cols = lax.dynamic_slice_in_dim(pat_rows, col_here * ac, ac, axis=1)
    keep_sq = mm(mm(e_rowb, here_cols).astype(BF), e_colt)
    square = (mm(m, right) * (s * s) * keep_sq).astype(BF)
    square = lax.all_gather(square, "row", axis=0, tiled=True)
    cube = lax.all_gather((mm(m, square) * s).astype(BF), "row", axis=0, tiled=True)
    start = (mm(pick_row, right) * s).astype(BF).astype(F32)
    keep_out = mm(mm(e_rowb, pattern.astype(BF)).astype(BF), e_colt)
    return keep_out * (1.5 * start - 0.5 * mm(pick_row, cube))


def solution(mesh):
    in_specs = (P("row", "col"), P(), P("row", "col"))
    out_specs = P("row", "col")
    return jax.shard_map(
        on_device, mesh=mesh, in_specs=in_specs, out_specs=out_specs, check_vma=False
    )
```

profile of v0, /device:TPU:0, one launch (start us, length us, event | category | flops | bytes accessed | tf_op | source)
XLA Modules:
  0.0 211.8 jit_solution(7994260219636314159)
XLA Ops:
  6.5 0.7 all-gather.14.cloned.1.call-update
  7.3 0.7 convert_bitcast_fusion
  8.0 75.1 %all-gather.2 = bf16[32,56,28]{1,2,0:T(8,128)(2,1)S(1)} all-gather(bf16[1,56,28]{1,2,0:T(8,128)(2,1)S(1)} %convert_bitcast_fusion), channel_id=2, replica_groups=mesh['row'=4,'col'=8] {'row','col'}, dimensions={0}, use_global_device_ids=true | all-gather | bytes 103488 | tf_op jit(solution)/shard_map/all_gather | solution.py:29
  83.2 0.2 copy.12
  83.3 0.2 reshape.30
  83.5 0.8 iota_subtract_fusion
  84.4 0.9 convolution_convert_fusion.5
  85.3 0.9 convolution_convert_fusion.4
  86.2 5.0 %all-gather.14.cloned.1.call-done = bf16[8,364,728]{1,2,0:T(8,128)(2,1)} async-done(((bf16[1,364,728]{1,2,0:T(8,128)(2,1)}), bf16[8,364,728]{1,2,0:T(8,128)(2,1)}) %all-gather.14.cloned.1.call-update) | async-done | bytes 4239888 | tf_op jit(solution)/shard_map/all_gather | solution.py:28
  91.2 4.9 %copy.9 = bf16[8,364,728]{1,0,2:T(8,128)(2,1)} copy(bf16[8,364,728]{1,2,0:T(8,128)(2,1)} %all-gather.14.cloned.1.call-done) | data formatting | bytes 8479744 | tf_op jit(solution)/shard_map/all_gather | solution.py:28
  96.1 8.6 %reshape.34 = bf16[2912,728]{0,1:T(8,128)(2,1)} reshape(bf16[8,364,728]{1,0,2:T(8,128)(2,1)} %copy.9) | data formatting | bytes 8479744
  104.7 6.9 %multiply_reduce_fusion = (f32[]{:T(128)}, bf16[728,2912]{1,0:T(8,128)(2,1)}) fusion(s32[224]{0:T(256)S(1)} %get-tuple-element.8, s32[224]{0:T(256)S(1)} %get-tuple-element.7, bf16[56,224]{1,0:T(8,128)(2,1)S(1)} %convolution_convert_fusion.4, s32[56]{0:T(128)S(1)} %get-tuple-element.10, s32[56]{0:T(128)S(1)} %get-tuple-element.9, bf16[2912,728]{0,1:T(8,128)(2,1)} %reshape.34), kind=kOutput, calls=%fused_computation | convolution fusion | flops 987197120 | bytes 8507076 | tf_op jit(solution)/shard_map/dot_general | solution.py:12
  111.6 5.5 %fusion.19 = bf16[728,364]{1,0:T(8,128)(2,1)} fusion(bf16[728,2912]{1,0:T(8,128)(2,1)} %get-tuple-element.6, s32[364]{0:T(512)S(1)} %iota_add_fusion.1), kind=kOutput, calls=%fused_computation.28 | convolution fusion | flops 1544638336 | bytes 4771312 | tf_op jit(solution)/shard_map/dot_general | solution.py:12
  117.2 6.2 %psum.7 = f32[]{:T(128)} all-reduce(f32[]{:T(128)} %get-tuple-element.5), channel_id=1, replica_groups=mesh['row'=4,'col'=8] {'row'}, use_global_device_ids=true, to_apply=%region_3.4 | all-reduce | flops 1 | bytes 8 | tf_op jit(solution)/shard_map/psum | solution.py:44
  124.2 15.2 %all-gather.8.cloned.1.call-done = bf16[2912,364]{1,0:T(8,128)(2,1)} async-done(((bf16[728,364]{1,0:T(8,128)(2,1)}), bf16[2912,364]{1,0:T(8,128)(2,1)}) %all-gather.8.cloned.1.call-update) | async-done | bytes 2119952 | tf_op jit(solution)/shard_map/all_gather | solution.py:57
  139.3 5.4 %convolution_multiply_fusion.1 = f32[728,364]{1,0:T(8,128)S(1)} fusion(bf16[728,2912]{1,0:T(8,128)(2,1)} %get-tuple-element.6, bf16[2912,364]{1,0:T(8,128)(2,1)} %all-gather.8.cloned.1.call-done, f32[]{:T(128)S(6)} %mul.104), kind=kOutput, calls=%fused_computation.17 | convolution fusion | flops 1543578368 | bytes 7419780 | tf_op jit(solution)/shard_map/dot_general | solution.py:12
  144.7 1.5 fusion.17
  146.2 0.2 all-gather.12.cloned.1.call-start
  146.5 23.3 %all-gather.10.cloned.1.call-done = bf16[2912,364]{1,0:T(8,128)(2,1)} async-done(((bf16[728,364]{1,0:T(8,128)(2,1)}), bf16[2912,364]{1,0:T(8,128)(2,1)}) %all-gather.10.cloned.1.call-update) | async-done | bytes 2119952 | tf_op jit(solution)/shard_map/all_gather | solution.py:62
  169.7 6.2 %fusion.18 = bf16[728,364]{1,0:T(8,128)(2,1)} fusion(bf16[728,2912]{1,0:T(8,128)(2,1)} %get-tuple-element.6, bf16[2912,364]{1,0:T(8,128)(2,1)} %all-gather.10.cloned.1.call-done, f32[]{:T(128)S(6)} %rsqrt.3), kind=kOutput, calls=%fused_computation.27 | convolution fusion | flops 1543843328 | bytes 6889796 | tf_op jit(solution)/shard_map/dot_general | solution.py:12
  176.2 2.5 %fusion.16 = f32[728,364]{1,0:T(8,128)S(1)} fusion(bf16[2912,364]{1,0:T(8,128)(2,1)S(1)} %copy-done.2, s32[728]{0:T(1024)S(1)} %iota_add_fusion, f32[]{:T(128)S(6)} %rsqrt.3), kind=kOutput, calls=%fused_computation.25 | convolution fusion | flops 1546493184 | bytes 3182820 | tf_op jit(solution)/shard_map/dot_general | solution.py:12
  178.7 20.7 %all-gather.12.cloned.1.call-done = bf16[2912,364]{1,0:T(8,128)(2,1)} async-done(((bf16[728,364]{1,0:T(8,128)(2,1)}), bf16[2912,364]{1,0:T(8,128)(2,1)}) %all-gather.12.cloned.1.call-update) | async-done | bytes 2119952 | tf_op jit(solution)/shard_map/all_gather | solution.py:63
  199.5 4.1 %fusion.13 = f32[728,364]{1,0:T(8,128)S(1)} fusion(f32[728,364]{1,0:T(8,128)S(1)} %fusion.16, bf16[2912,364]{1,0:T(8,128)(2,1)} %all-gather.12.cloned.1.call-done, s32[728]{0:T(1024)S(1)} %iota_add_fusion), kind=kOutput, calls=%fused_computation.22 | convolution fusion | flops 1545963264 | bytes 4242784 | tf_op jit(solution)/shard_map/dot_general | solution.py:12
  203.6 1.6 convolution_multiply_fusion.3
  (21 shorter events, 0.5 us)
Async XLA Ops:
  6.5 84.7 %all-gather.14.cloned.1.call-start = ((), (), s32[]{:S(2)}) async-start(), calls=%async_computation.3 | async-start | bytes 5031936 | tf_op jit(solution)/shard_map/all_gather | solution.py:28
  7.3 132.1 %all-gather.8.cloned.1.call-start = ((), (), s32[]{:S(2)}) async-start(), calls=%async_computation | async-start | bytes 2795520 | tf_op jit(solution)/shard_map/all_gather | solution.py:57
  117.1 52.6 %all-gather.10.cloned.1.call-start = ((), (), s32[]{:S(2)}) async-start(), calls=%async_computation.1 | async-start | bytes 2795520 | tf_op jit(solution)/shard_map/all_gather | solution.py:62
  146.2 29.8 %copy-start.1 = (s32[224]{0:T(256)S(1)}, s32[224]{0:T(256)}, u32[]{:S(2)}) copy-start(s32[224]{0:T(256)} %param.4) | copy-start | bytes 2692
  146.2 30.0 %copy-start.2 = (bf16[2912,364]{1,0:T(8,128)(2,1)S(1)}, bf16[2912,364]{1,0:T(8,128)(2,1)}, u32[]{:S(2)}) copy-start(bf16[2912,364]{1,0:T(8,128)(2,1)} %all-gather.8.cloned.1.call-done) | copy-start | bytes 6359812
  146.2 53.2 %all-gather.12.cloned.1.call-start = ((), (), s32[]{:S(2)}) async-start(), calls=%async_computation.2 | async-start | bytes 2795520 | tf_op jit(solution)/shard_map/all_gather | solution.py:63
  178.7 24.9 %copy-start = (s32[56,28]{0,1:T(8,128)S(1)}, s32[56,28]{0,1:T(8,128)}, u32[]{:S(2)}) copy-start(s32[56,28]{0,1:T(8,128)} %param.5) | copy-start | bytes 18820
Sparse Core Ops, SparseCore 0:
  9.5 81.6 all-gather.13
  117.2 22.0 all-gather.7
  146.3 23.3 all-gather.9
  176.1 23.3 all-gather.11
where the time goes:
time: 212 us
  blocking collectives  81.4 us (38%)
  waiting for transfers between devices  64.9 us (31%)
  matrix products  35.5 us (17%)
  between operations  14 us (7%)
  local copies, waits for them, and re-layouts  13.8 us (7%)
    all_gather x1, blocking collectives, on_device(): lax.all_gather(pattern.astype(BF), ('row', 'col'), axis=0, tiled=False)  75.1 us
    dot_general x10, matrix products, mm(): return jnp.dot(a, b, preferred_element_type=F32)  35.5 us
    all_gather x1, waiting for transfers between devices, on_device(): square = lax.all_gather(square, 'row', axis=0, tiled=True)  23.3 us
    all_gather x1, waiting for transfers between devices, on_device(): lax.all_gather((mm(m, square) * s).astype(BF), 'row', axis=0, tiled=True)  20.7 us
    all_gather x1, waiting for transfers between devices, on_device(): lax.all_gather(mm(m, pick_col).astype(BF), 'row', axis=0, tiled=True)  15.2 us
    unnamed x7, local copies, waits for them, and re-layouts  8.62 us
    psum x1, blocking collectives, on_device(): total = lax.psum(jnp.sum(m.astype(F32) ** 2), 'row')  6.25 us
    all_gather x1, waiting for transfers between devices, on_device(): panel = lax.all_gather(hamiltonian, 'col', axis=1, tiled=True)  5 us
  transfers between devices with their start and end apart: 4, of which 4 were waited for; matrix products, arithmetic and copies ran while one was open for 3% of the time, Pallas kernels for 0%

commit v1 on v0

--- a/solution.py
+++ b/solution.py
@@ -59,7 +59,12 @@
     here_cols = lax.dynamic_slice_in_dim(pat_rows, col_here * ac, ac, axis=1)
     keep_sq = mm(mm(e_rowb, here_cols).astype(BF), e_colt)
     square = (mm(m, right) * (s * s) * keep_sq).astype(BF)
-    square = lax.all_gather(square, "row", axis=0, tiled=True)
+    ring = [square]
+    for hop in range(3):
+        ring.append(lax.ppermute(ring[-1], "row", [(dev, (dev + 1) % 4) for dev in range(4)]))
+    square = jnp.roll(
+        jnp.concatenate(ring[::-1], axis=0), (lax.axis_index("row") + 1) * ring[0].shape[0], axis=0
+    )
     cube = lax.all_gather((mm(m, square) * s).astype(BF), "row", axis=0, tiled=True)
     start = (mm(pick_row, right) * s).astype(BF).astype(F32)
     keep_out = mm(mm(e_rowb, pattern.astype(BF)).astype(BF), e_colt)

time: 212 us -> 215 us (1.014)
  waiting for transfers between devices: 64.9 us -> 68.4 us
    ppermute x0 -> x3, waiting for transfers between devices: none -> 26.7 us  [on_device(): lax.ppermute(ring[-1], 'row', [(dev, (dev + 1) % 4) for dev in range(4)])]
    all_gather x1 -> x0, waiting for transfers between devices: 23.3 us -> none  [on_device(): square = lax.all_gather(square, 'row', axis=0, tiled=True)]
    unnamed x7 -> x14, local copies, waits for them, and re-layouts: 8.62 us -> 9.22 us
  transfers between devices with their start and end apart: 4 -> 6, of which waited for: 4 -> 6; matrix products, arithmetic and copies ran while one was open for 3% -> 3% of each run, Pallas kernels for 0% -> 0%
where the time goes in v1:
time: 215 us
  blocking collectives  81.4 us (38%)
  waiting for transfers between devices  68.4 us (32%)
  matrix products  34.2 us (16%)
  local copies, waits for them, and re-layouts  14.5 us (7%)
  between operations  14 us (7%)
    all_gather x1, blocking collectives, on_device(): lax.all_gather(pattern.astype(BF), ('row', 'col'), axis=0, tiled=False)  75.1 us
    dot_general x10, matrix products, mm(): return jnp.dot(a, b, preferred_element_type=F32)  34.2 us
    ppermute x3, waiting for transfers between devices, on_device(): lax.ppermute(ring[-1], 'row', [(dev, (dev + 1) % 4) for dev in range(4)])  26.7 us
    all_gather x1, waiting for transfers between devices, on_device(): lax.all_gather((mm(m, square) * s).astype(BF), 'row', axis=0, tiled=True)  20.7 us
    all_gather x1, waiting for transfers between devices, on_device(): lax.all_gather(mm(m, pick_col).astype(BF), 'row', axis=0, tiled=True)  15.2 us
    unnamed x14, local copies, waits for them, and re-layouts  9.22 us
    psum x1, blocking collectives, on_device(): total = lax.psum(jnp.sum(m.astype(F32) ** 2), 'row')  6.25 us
    all_gather x1, waiting for transfers between devices, on_device(): panel = lax.all_gather(hamiltonian, 'col', axis=1, tiled=True)  5 us
  transfers between devices with their start and end apart: 6, of which 6 were waited for; matrix products, arithmetic and copies ran while one was open for 3% of the time, Pallas kernels for 0%

profile of v1, /device:TPU:0, one launch (start us, length us, event | category | flops | bytes accessed | tf_op | source)
XLA Modules:
  0.0 214.7 jit_solution(2861606941111251633)
XLA Ops:
  6.5 0.7 all-gather.11.cloned.1.call-update
  7.3 0.7 convert_bitcast_fusion
  8.0 75.1 %all-gather.2 = bf16[32,56,28]{1,2,0:T(8,128)(2,1)S(1)} all-gather(bf16[1,56,28]{1,2,0:T(8,128)(2,1)S(1)} %convert_bitcast_fusion), channel_id=2, replica_groups=mesh['row'=4,'col'=8] {'row','col'}, dimensions={0}, use_global_device_ids=true | all-gather | bytes 103488 | tf_op jit(solution)/shard_map/all_gather | solution.py:29
  83.5 0.8 iota_subtract_fusion
  84.4 0.9 convolution_convert_fusion.5
  85.3 0.9 convolution_convert_fusion.4
  86.2 5.0 %all-gather.11.cloned.1.call-done = bf16[8,364,728]{1,2,0:T(8,128)(2,1)} async-done(((bf16[1,364,728]{1,2,0:T(8,128)(2,1)}), bf16[8,364,728]{1,2,0:T(8,128)(2,1)}) %all-gather.11.cloned.1.call-update) | async-done | bytes 4239888 | tf_op jit(solution)/shard_map/all_gather | solution.py:28
  91.2 4.9 %copy.9 = bf16[8,364,728]{1,0,2:T(8,128)(2,1)} copy(bf16[8,364,728]{1,2,0:T(8,128)(2,1)} %all-gather.11.cloned.1.call-done) | data formatting | bytes 8479744 | tf_op jit(solution)/shard_map/all_gather | solution.py:28
  96.1 8.6 %reshape.34 = bf16[2912,728]{0,1:T(8,128)(2,1)} reshape(bf16[8,364,728]{1,0,2:T(8,128)(2,1)} %copy.9) | data formatting | bytes 8479744
  104.7 6.9 %multiply_reduce_fusion = (f32[]{:T(128)}, bf16[728,2912]{1,0:T(8,128)(2,1)}) fusion(s32[224]{0:T(256)S(1)} %get-tuple-element.8, s32[224]{0:T(256)S(1)} %get-tuple-element.7, bf16[56,224]{1,0:T(8,128)(2,1)S(1)} %convolution_convert_fusion.4, s32[56]{0:T(128)S(1)} %get-tuple-element.10, s32[56]{0:T(128)S(1)} %get-tuple-element.9, bf16[2912,728]{0,1:T(8,128)(2,1)} %reshape.34), kind=kOutput, calls=%fused_computation | convolution fusion | flops 987197120 | bytes 8507076 | tf_op jit(solution)/shard_map/dot_general | solution.py:12
  111.6 5.5 %fusion.26 = bf16[728,364]{1,0:T(8,128)(2,1)} fusion(bf16[728,2912]{1,0:T(8,128)(2,1)} %get-tuple-element.6, s32[364]{0:T(512)S(1)} %iota_add_fusion.1), kind=kOutput, calls=%fused_computation.30 | convolution fusion | flops 1544638336 | bytes 4771312 | tf_op jit(solution)/shard_map/dot_general | solution.py:12
  117.2 6.2 %psum.7 = f32[]{:T(128)} all-reduce(f32[]{:T(128)} %get-tuple-element.5), channel_id=1, replica_groups=mesh['row'=4,'col'=8] {'row'}, use_global_device_ids=true, to_apply=%region_3.4 | all-reduce | flops 1 | bytes 8 | tf_op jit(solution)/shard_map/psum | solution.py:44
  124.2 15.2 %all-gather.7.cloned.1.call-done = bf16[2912,364]{1,0:T(8,128)(2,1)} async-done(((bf16[728,364]{1,0:T(8,128)(2,1)}), bf16[2912,364]{1,0:T(8,128)(2,1)}) %all-gather.7.cloned.1.call-update) | async-done | bytes 2119952 | tf_op jit(solution)/shard_map/all_gather | solution.py:57
  139.3 5.4 %convolution_multiply_fusion = f32[728,364]{1,0:T(8,128)S(1)} fusion(bf16[728,2912]{1,0:T(8,128)(2,1)} %get-tuple-element.6, bf16[2912,364]{1,0:T(8,128)(2,1)} %all-gather.7.cloned.1.call-done, f32[]{:T(128)S(6)} %mul.107), kind=kOutput, calls=%fused_computation.18 | convolution fusion | flops 1543578368 | bytes 7419780 | tf_op jit(solution)/shard_map/dot_general | solution.py:12
  144.7 0.7 fusion.22
  145.4 0.3 collective-permute-start
  145.7 8.8 %collective-permute-done = bf16[728,364]{1,0:T(8,128)(2,1)S(1)} collective-permute-done((bf16[728,364]{1,0:T(8,128)(2,1)S(1)}, bf16[728,364]{1,0:T(8,128)(2,1)S(1)}, u32[]{:S(2)}, u32[]{:S(2)}) %collective-permute-start) | collective-permute-done | bytes 530016 | tf_op jit(solution)/shard_map/ppermute | solution.py:64
  154.4 9.0 %collective-permute-done.1 = bf16[728,364]{1,0:T(8,128)(2,1)S(1)} collective-permute-done((bf16[728,364]{1,0:T(8,128)(2,1)S(1)}, bf16[728,364]{1,0:T(8,128)(2,1)S(1)}, u32[]{:S(2)}, u32[]{:S(2)}) %collective-permute-start.1) | collective-permute-done | bytes 530016 | tf_op jit(solution)/shard_map/ppermute | solution.py:64
  163.4 9.0 %collective-permute-done.2 = bf16[728,364]{1,0:T(8,128)(2,1)S(1)} collective-permute-done((bf16[728,364]{1,0:T(8,128)(2,1)S(1)}, bf16[728,364]{1,0:T(8,128)(2,1)S(1)}, u32[]{:S(2)}, u32[]{:S(2)}) %collective-permute-start.2) | collective-permute-done | bytes 530016 | tf_op jit(solution)/shard_map/ppermute | solution.py:64
  173.2 5.7 %fusion.23 = bf16[728,364]{1,0:T(8,128)(2,1)} fusion(bf16[728,2912]{1,0:T(8,128)(2,1)} %get-tuple-element.6, bf16[5824,364]{1,0:T(8,128)(2,1)S(1)} %constant_dynamic-update-slice_fusion, s32[]{:T(128)S(6)} %select_n.33, f32[]{:T(128)S(6)} %rsqrt.3), kind=kOutput, calls=%fused_computation.29 | convolution fusion | flops 1543843328 | bytes 7006280 | tf_op jit(solution)/shard_map/dot_general | solution.py:12
  179.1 2.5 %fusion.21 = f32[728,364]{1,0:T(8,128)S(1)} fusion(bf16[2912,364]{1,0:T(8,128)(2,1)S(1)} %copy-done.2, s32[728]{0:T(1024)S(1)} %iota_add_fusion, f32[]{:T(128)S(6)} %rsqrt.3), kind=kOutput, calls=%fused_computation.27 | convolution fusion | flops 1546493184 | bytes 3182820 | tf_op jit(solution)/shard_map/dot_general | solution.py:12
  181.6 20.7 %all-gather.9.cloned.1.call-done = bf16[2912,364]{1,0:T(8,128)(2,1)} async-done(((bf16[728,364]{1,0:T(8,128)(2,1)}), bf16[2912,364]{1,0:T(8,128)(2,1)}) %all-gather.9.cloned.1.call-update) | async-done | bytes 2119952 | tf_op jit(solution)/shard_map/all_gather | solution.py:68
  202.4 4.1 %fusion.18 = f32[728,364]{1,0:T(8,128)S(1)} fusion(f32[728,364]{1,0:T(8,128)S(1)} %fusion.21, bf16[2912,364]{1,0:T(8,128)(2,1)} %all-gather.9.cloned.1.call-done, s32[728]{0:T(1024)S(1)} %iota_add_fusion), kind=kOutput, calls=%fused_computation.24 | convolution fusion | flops 1545963264 | bytes 4242784 | tf_op jit(solution)/shard_map/dot_general | solution.py:12
  206.5 1.6 convolution_multiply_fusion.2
  (32 shorter events, 1.5 us)
Async XLA Ops:
  6.5 84.7 %all-gather.11.cloned.1.call-start = ((), (), s32[]{:S(2)}) async-start(), calls=%async_computation.2 | async-start | bytes 5031936 | tf_op jit(solution)/shard_map/all_gather | solution.py:28
  7.3 132.1 %all-gather.7.cloned.1.call-start = ((), (), s32[]{:S(2)}) async-start(), calls=%async_computation | async-start | bytes 2795520 | tf_op jit(solution)/shard_map/all_gather | solution.py:57
  117.1 85.3 %all-gather.9.cloned.1.call-start = ((), (), s32[]{:S(2)}) async-start(), calls=%async_computation.1 | async-start | bytes 2795520 | tf_op jit(solution)/shard_map/all_gather | solution.py:68
  145.4 9.0 %collective-permute-start = (bf16[728,364]{1,0:T(8,128)(2,1)S(1)}, bf16[728,364]{1,0:T(8,128)(2,1)S(1)}, u32[]{:S(2)}, u32[]{:S(2)}) collective-permute-start(bf16[728,364]{1,0:T(8,128)(2,1)S(1)} %fusion.22), channel_id=1, source_target_pairs={{0,8},{8,16},{16,24},{24,0},{1,9},{9,17},{17,25},{25,1},{2,10},{10... | collective-permute-start | bytes 1589960 | tf_op jit(solution)/shard_map/ppermute | solution.py:64
  154.4 9.0 %collective-permute-start.1 = (bf16[728,364]{1,0:T(8,128)(2,1)S(1)}, bf16[728,364]{1,0:T(8,128)(2,1)S(1)}, u32[]{:S(2)}, u32[]{:S(2)}) collective-permute-start(bf16[728,364]{1,0:T(8,128)(2,1)S(1)} %collective-permute-done), channel_id=1, source_target_pairs={{0,8},{8,16},{16,24},{24,0},{1,9},{9,17},{17,25},{25,1},{2,10},{10... | collective-permute-start | bytes 1589960 | tf_op jit(solution)/shard_map/ppermute | solution.py:64
  163.4 9.0 %collective-permute-start.2 = (bf16[728,364]{1,0:T(8,128)(2,1)S(1)}, bf16[728,364]{1,0:T(8,128)(2,1)S(1)}, u32[]{:S(2)}, u32[]{:S(2)}) collective-permute-start(bf16[728,364]{1,0:T(8,128)(2,1)S(1)} %collective-permute-done.1), channel_id=1, source_target_pairs={{0,8},{8,16},{16,24},{24,0},{1,9},{9,17},{17,25},{25,1},{2,10},{10... | collective-permute-start | bytes 1589960 | tf_op jit(solution)/shard_map/ppermute | solution.py:64
  173.1 5.7 %copy-start.1 = (s32[224]{0:T(256)S(1)}, s32[224]{0:T(256)}, u32[]{:S(2)}) copy-start(s32[224]{0:T(256)} %param.4) | copy-start | bytes 2692
  173.1 5.9 %copy-start.2 = (bf16[2912,364]{1,0:T(8,128)(2,1)S(1)}, bf16[2912,364]{1,0:T(8,128)(2,1)}, u32[]{:S(2)}) copy-start(bf16[2912,364]{1,0:T(8,128)(2,1)} %all-gather.7.cloned.1.call-done) | copy-start | bytes 6359812
  181.6 24.9 %copy-start = (s32[56,28]{0,1:T(8,128)S(1)}, s32[56,28]{0,1:T(8,128)}, u32[]{:S(2)}) copy-start(s32[56,28]{0,1:T(8,128)} %param.5) | copy-start | bytes 18820
Sparse Core Ops, SparseCore 0:
  9.5 81.6 all-gather.10
  117.2 22.0 all-gather.6
  179.0 23.3 all-gather.8
